TPU v7x, 256 devices: a whole 4x4x8 slice. The times are simulated.
256 devices in a mesh: blk: 128 (over x, z, y), row: 2 (over core).
Axes of the slice: x: 4, y: 4, z: 8, core: 2. Of those that a mesh axis runs over, the one named last changes fastest.
Arguments:
- genotypes: bfloat16 [1024, 128, 2048], P('blk', None, 'row'), may hold values from 0 to 2
- assignment: int32 [128], replicated, may hold values from 0 to 127, each once
- snp_counts: int32 [128], replicated, may hold values from 1024 to 2048, as said below
- basis: float32 [128, 64, 2048], P('blk', None, 'row'), may hold values from -6 to 6
Outputs:
- image: float32 [128, 64, 2048], P('blk', None, 'row')
- new_basis: float32 [128, 64, 2048], P('blk', None, 'row')
- factor: float32 [128, 64, 64], P('blk')
Inputs may be any that keep to these rules, and one draw needn't show every extreme that they name: `assignment`: each block number appears exactly once. `snp_counts`: A block's SNPs fill its leading slots.
All inputs are finite; a program needn't handle non-finite values.
Results may differ from a plain program's by a relative error of at most 0.0021.
Values may be sent and summed in bfloat16 or wider, within the bound.
A program may use at most 64 MiB of HBM per device.

v0:
```python
import jax
import jax.numpy as jnp
from jax import lax
from jax.sharding import PartitionSpec as P

epsilon = 1e-05
shrink_weight = 0.5


def total_of_pieces(array, axis):
    pieces = lax.all_gather(array, axis)
    return pieces.sum(axis=0)


def body(genotypes, assignment, snp_counts, basis):
    ordered = jnp.take(genotypes, assignment, axis=1)
    regrouped = lax.all_to_all(ordered, "blk", split_axis=1, concat_axis=0, tiled=True)
    samples = regrouped.shape[0]
    owned = regrouped.shape[1]
    half_width = regrouped.shape[2]
    block_ids = lax.dynamic_slice_in_dim(assignment, lax.axis_index("blk") * owned, owned)
    catalog = jnp.arange(snp_counts.shape[0], dtype=jnp.int32)
    live_count = jnp.sum(
        jnp.where(block_ids[:, None] == catalog[None, :], snp_counts[None, :], 0), axis=1
    )
    columns = lax.axis_index("row") * half_width + jnp.arange(half_width, dtype=jnp.int32)
    live_mask = columns[None, :] < live_count[:, None]
    values = regrouped.astype(jnp.float32)
    col_mean = jnp.mean(values, axis=0)
    centered = values - col_mean[None]
    col_var = jnp.mean(centered * centered, axis=0)
    standard = jnp.where(
        live_mask[None], centered * lax.rsqrt(col_var + epsilon)[None], 0.0
    ).astype(jnp.bfloat16)
    inverse = 1.0 / samples
    partial_proj = jnp.einsum(
        "nbi,bri->brn",
        standard,
        basis,
        precision=lax.Precision.HIGHEST,
        preferred_element_type=jnp.float32,
    )
    projected = total_of_pieces(partial_proj, "row")
    product = (
        jnp.einsum(
            "nbi,brn->bri",
            standard,
            projected,
            precision=lax.Precision.HIGHEST,
            preferred_element_type=jnp.float32,
        )
        * inverse
    )
    image = shrink_weight * product + (1.0 - shrink_weight) * jnp.where(
        live_mask[:, None, :], basis, 0.0
    )
    gram_part = jnp.einsum("bri,bsi->brs", image, image, precision=lax.Precision.HIGHEST)
    gram_sum = total_of_pieces(gram_part, "row")
    factor = jnp.linalg.cholesky(gram_sum)
    new_basis = jax.scipy.linalg.solve_triangular(factor, image, lower=True)
    return (image, new_basis, factor)


def solution(mesh):
    in_specs = (P("blk", None, "row"), P(), P(), P("blk", None, "row"))
    out_specs = (P("blk", None, "row"), P("blk", None, "row"), P("blk", None, None))
    return jax.shard_map(body, mesh=mesh, in_specs=in_specs, out_specs=out_specs, check_vma=False)
```

profile of v0, /device:TPU:1, one launch (start us, length us, event | category | flops | bytes accessed | tf_op | source)
XLA Modules:
  0.0 113.4 jit_solution(6416810635120617516)
XLA Ops:
  0.6 0.0 copy-start
  0.6 0.8 compare_select_fusion
  1.5 0.7 compare_and_fusion
  2.1 0.1 copy-done
  2.2 8.1 %gather_fusion = bf16[128,8,1024]{2,0,1:T(8,128)(2,1)} fusion(bf16[8,128,1024]{2,1,0:T(8,128)(2,1)S(1)} %copy-done, s32[1024]{0:T(1024)S(1)} %pad_clamp_fusion), kind=kCustom, calls=%fused_computation | custom fusion | bytes 4194816 | tf_op jit(solution)/shard_map/jit(_take)/gather | solution.py:16
  10.3 1.8 %select_bitcast_fusion = bf16[8,128,1024]{2,1,0:T(8,128)(2,1)S(1)} fusion(bf16[128,8,1024]{2,0,1:T(8,128)(2,1)} %gather_fusion, pred[128]{0:T(512)(128)(4,1)S(1)} %compare_and_fusion), kind=kLoop, calls=%fused_computation.18 | loop fusion | flops 1048576 | bytes 4194432 | tf_op jit(solution)/shard_map/jit(_take)/select_n | solution.py:16
  12.1 2.4 %copy.12 = bf16[8,128,1024]{2,0,1:T(8,128)(2,1)} copy(bf16[8,128,1024]{2,1,0:T(8,128)(2,1)S(1)} %select_bitcast_fusion) | data formatting | bytes 4194304 | tf_op jit(solution)/shard_map/jit(_take)/select_n | solution.py:16
  14.6 17.2 %all-to-all-start = ((bf16[8,128,1024]{2,0,1:T(8,128)(2,1)}), bf16[8,128,1024]{2,0,1:T(8,128)(2,1)}, u32[]{:S(2)}, u32[]{:S(2)}) async-start(bf16[8,128,1024]{2,0,1:T(8,128)(2,1)} %copy.12), calls=%async_computation | async-start | bytes 4194304 | tf_op jit(solution)/shard_map/all_to_all | solution.py:17
  31.8 0.0 copy-done.3
  31.8 0.6 dynamic_slice.3
  32.4 0.0 copy-done.4
  32.4 1.3 %fusion.40 = s32[]{:T(128)} fusion(s32[128]{0:T(128)S(1)} %copy-done.4, s32[]{:T(128)} %bitcast), kind=kLoop, calls=%fused_computation.50 | loop fusion | flops 383 | bytes 520 | tf_op jit(solution)/shard_map/reduce_sum | solution.py:23
  33.7 0.7 add_compare_fusion
  34.3 0.0 copy-start.2
  34.3 46.3 %all-to-all-done = bf16[8,128,1024]{2,0,1:T(8,128)(2,1)} async-done(((bf16[8,128,1024]{2,0,1:T(8,128)(2,1)}), bf16[8,128,1024]{2,0,1:T(8,128)(2,1)}, u32[]{:S(2)}, u32[]{:S(2)}) %all-to-all-start) | async-done | bytes 2097184 | tf_op jit(solution)/shard_map/all_to_all | solution.py:17
  80.6 2.0 %convert_reduce_fusion = f32[1024]{0:T(1024)S(1)} fusion(bf16[8,128,1024]{2,0,1:T(8,128)(2,1)} %all-to-all-done), kind=kLoop, calls=%fused_computation.3 | loop fusion | flops 2096128 | bytes 2101248 | tf_op jit(solution)/shard_map/reduce_sum | solution.py:29
  82.6 2.2 %fusion.10 = f32[1024]{0:T(1024)S(1)} fusion(bf16[8,128,1024]{2,0,1:T(8,128)(2,1)} %all-to-all-done, f32[1024]{0:T(1024)S(1)} %broadcast_multiply_fusion), kind=kLoop, calls=%fused_computation.15 | loop fusion | flops 4193280 | bytes 2105344 | tf_op jit(solution)/shard_map/reduce_sum | solution.py:31
  84.8 0.0 copy-done.2
  84.8 3.6 %fusion.21 = f32[64,1024]{1,0:T(8,128)S(1)} fusion(bf16[8,128,1024]{2,0,1:T(8,128)(2,1)} %all-to-all-done, f32[1024]{0:T(1024)S(1)} %add_rsqrt_fusion, f32[1024]{0:T(1024)S(1)} %broadcast_multiply_fusion, pred[1024]{0:T(1024)(128)(4,1)S(1)} %add_compare_fusion, f32[1,64,1024]{2,1,0:T(8,128)S(1)} %copy-done.2), kind=kOutput, calls=%fused_computation.26 | convolution fusion | flops 810549248 | bytes 2630656 | tf_op jit(solution)/shard_map/nbi,bri->brn/dot_general | solution.py:36
  88.4 5.7 %all-gather = f32[128,1024]{1,0:T(8,128)S(1)} all-gather(f32[64,1024]{1,0:T(8,128)S(1)} %fusion.21), channel_id=2, replica_groups=mesh['blk'=128,'row'=2] {'row'}, dimensions={0}, use_global_device_ids=true | all-gather | bytes 786432 | tf_op jit(solution)/shard_map/all_gather | solution.py:11
  94.1 3.0 %fusion.30 = f32[1,64,1024]{2,1,0:T(8,128)S(1)} fusion(f32[64,1024]{1,0:T(8,128)S(1)} %reduce.18, bf16[8,128,1024]{2,0,1:T(8,128)(2,1)} %all-to-all-done, f32[1024]{0:T(1024)S(1)} %add_rsqrt_fusion, f32[1024]{0:T(1024)S(1)} %broadcast_multiply_fusion, pred[1024]{0:T(1024)(128)(4,1)S(1)} %add_compare_fusion, f32[1,64,1024]{2,1,0:T(8,128)S(1)} %copy-done.2), kind=kOutput, calls=%fused_computation.29 | convolution fusion | flops 810811392 | bytes 2892800 | tf_op jit(solution)/shard_map/nbi,brn->bri/dot_general | solution.py:45
  97.1 0.0 copy-start.1
  97.1 0.4 fusion.34
  97.5 1.9 %all-gather.1 = f32[128,64]{1,0:T(8,128)S(1)} all-gather(f32[64,64]{1,0:T(8,128)S(1)} %fusion.34), channel_id=3, replica_groups=mesh['blk'=128,'row'=2] {'row'}, dimensions={0}, use_global_device_ids=true | all-gather | bytes 49152 | tf_op jit(solution)/shard_map/all_gather | solution.py:11
  99.4 0.1 copy.13
  99.5 0.1 copy.14
  99.6 5.8 %custom-call.8 = f32[1,64,64]{2,1,0:T(8,128)S(1)} custom-call(f32[1,64,64]{2,1,0:T(8,128)S(1)} %fusion.37), custom_call_target="Cholesky" | custom-call | tf_op jit(solution)/shard_map/jit(cholesky)/cholesky | solution.py:59
  105.4 0.6 compare_reduce_fusion
  106.1 1.3 %fusion.39 = (f32[1,64,64]{2,1,0:T(8,128)S(1)}, f32[1,64,64]{2,1,0:T(8,128)}) fusion(f32[1,64,64]{2,1,0:T(8,128)S(1)} %custom-call.8, pred[]{:T(512)} %compare_reduce_fusion), kind=kLoop, calls=%fused_computation.41 | loop fusion | flops 16384 | bytes 49153 | tf_op jit(solution)/shard_map/jit(_solve_triangular)/triangular_solve | solution.py:60
  107.4 4.9 %custom-call.9 = f32[1,64,64]{1,2,0:T(8,128)S(1)} custom-call(f32[1,64,64]{2,1,0:T(8,128)S(1)} %get-tuple-element.3), custom_call_target="InvertDiagBlocksLowerTriangular" | custom-call | tf_op jit(solution)/shard_map/jit(_solve_triangular)/triangular_solve | solution.py:60
  112.3 1.1 %convolution_bitcast_fusion = f32[1,64,1024]{2,1,0:T(8,128)} fusion(f32[1,64,1024]{2,1,0:T(8,128)S(1)} %fusion.30, f32[1,64,64]{1,2,0:T(8,128)S(1)} %custom-call.9), kind=kOutput, calls=%fused_computation.25 | convolution fusion | flops 50331648 | bytes 540672 | tf_op jit(solution)/shard_map/jit(_solve_triangular)/triangular_solve | solution.py:60
  113.4 0.0 copy-done.1
  (9 shorter events, 0.1 us)
Async XLA Ops:
  0.6 1.6 %copy-start = (bf16[8,128,1024]{2,1,0:T(8,128)(2,1)S(1)}, bf16[8,128,1024]{2,1,0:T(8,128)(2,1)}, u32[]{:S(2)}) copy-start(bf16[8,128,1024]{2,1,0:T(8,128)(2,1)} %param.4) | copy-start | bytes 6291460
  14.6 17.2 %copy-start.3 = (s32[128]{0:T(128)S(1)}, s32[128]{0:T(128)}, u32[]{:S(2)}) copy-start(s32[128]{0:T(128)} %param.5) | copy-start | bytes 1540
  14.6 17.8 %copy-start.4 = (s32[128]{0:T(128)S(1)}, s32[128]{0:T(128)}, u32[]{:S(2)}) copy-start(s32[128]{0:T(128)} %param.6) | copy-start | bytes 1540
  14.6 66.0 %all-to-all-start = ((bf16[8,128,1024]{2,0,1:T(8,128)(2,1)}), bf16[8,128,1024]{2,0,1:T(8,128)(2,1)}, u32[]{:S(2)}, u32[]{:S(2)}) async-start(bf16[8,128,1024]{2,0,1:T(8,128)(2,1)} %copy.12), calls=%async_computation | async-start | bytes 4194304 | tf_op jit(solution)/shard_map/all_to_all | solution.py:17
  34.3 50.5 %copy-start.2 = (f32[1,64,1024]{2,1,0:T(8,128)S(1)}, f32[1,64,1024]{2,1,0:T(8,128)}, u32[]{:S(2)}) copy-start(f32[1,64,1024]{2,1,0:T(8,128)} %param.7) | copy-start | bytes 786436
  97.1 16.3 %copy-start.1 = (f32[1,64,1024]{2,1,0:T(8,128)}, f32[1,64,1024]{2,1,0:T(8,128)S(1)}, u32[]{:S(2)}) copy-start(f32[1,64,1024]{2,1,0:T(8,128)S(1)} %fusion.30) | copy-start | bytes 786436
where the time goes:
time: 114 us; the launch traced here: 113 us
  waiting for transfers between devices  46.3 us (41%)
  other arithmetic  22.1 us (19%)
  starting transfers between devices  17.2 us (15%)
  local copies, waits for them, and re-layouts  11.4 us (10%)
  matrix products  8.12 us (7%)
  blocking collectives  7.54 us (7%)
    all_to_all x1, waiting for transfers between devices, body(): lax.all_to_all(ordered, 'blk', split_axis=1, concat_axis=0, tiled=True)  46.3 us
    all_to_all x1, starting transfers between devices, body(): lax.all_to_all(ordered, 'blk', split_axis=1, concat_axis=0, tiled=True)  17.2 us
    gather x1, local copies, waits for them, and re-layouts, body(): ordered = jnp.take(genotypes, assignment, axis=1)  8.06 us
    all_gather x2, blocking collectives, total_of_pieces(): pieces = lax.all_gather(array, axis)  7.54 us
    another operation x3, other arithmetic, body(): factor = jnp.linalg.cholesky(gram_sum)  6.52 us
    another operation x2, other arithmetic, body(): new_basis = jax.scipy.linalg.solve_triangular(factor, image, lower=True)  6.16 us
    dot_general x1, matrix products, body(): jnp.einsum('nbi,bri->brn', standard, basis, precision=lax.Precision.HIGHE...  3.61 us
    dot_general x1, matrix products, body(): jnp.einsum('nbi,brn->bri', standard, projected, precision=lax.Precision.H...  3.02 us
  transfers between devices with their start and end apart: 1, of which 1 were waited for; matrix products, arithmetic and copies ran while one was open for 2% of the time, Pallas kernels for 0%

commit v1 on v0

--- a/solution.py
+++ b/solution.py
@@ -14,7 +14,10 @@
 
 def body(genotypes, assignment, snp_counts, basis):
     ordered = jnp.take(genotypes, assignment, axis=1)
-    regrouped = lax.all_to_all(ordered, "blk", split_axis=1, concat_axis=0, tiled=True)
+    regrouped = jnp.concatenate(
+        lax.all_to_all(jnp.stack(jnp.split(ordered, lax.axis_size("blk"), axis=1)), "blk", 0, 0),
+        axis=0,
+    )
     samples = regrouped.shape[0]
     owned = regrouped.shape[1]
     half_width = regrouped.shape[2]

time: 114 us -> 194 us (1.70)
  local copies, waits for them, and re-layouts: 11.4 us -> 91 us
    unnamed x10 -> x137, local copies, waits for them, and re-layouts: 0.15 us -> 77.1 us
    split x0 -> x7, local copies, waits for them, and re-layouts: none -> 4.45 us  [body(): jnp.split(ordered, lax.axis_size('blk'), axis=1)]
    select_n x1 -> x0, local copies, waits for them, and re-layouts: 2.45 us -> none  [body(): ordered = jnp.take(genotypes, assignment, axis=1)]
  transfers between devices with their start and end apart: 1 -> 1, of which waited for: 1 -> 1; matrix products, arithmetic and copies ran while one was open for 2% -> 1% of each run, Pallas kernels for 0% -> 0%
where the time goes in v1:
time: 194 us; the launch traced here: 193 us
  local copies, waits for them, and re-layouts  91 us (47%)
  waiting for transfers between devices  46.5 us (24%)
  other arithmetic  22.1 us (11%)
  starting transfers between devices  17 us (9%)
  matrix products  8.13 us (4%)
  blocking collectives  7.53 us (4%)
    unnamed x137, local copies, waits for them, and re-layouts  77.1 us
    all_to_all x1, waiting for transfers between devices, body(): lax.all_to_all(jnp.stack(jnp.split(ordered, lax.axis_size('blk'), axis=1)...  46.5 us
    all_to_all x1, starting transfers between devices, body(): lax.all_to_all(jnp.stack(jnp.split(ordered, lax.axis_size('blk'), axis=1)...  17 us
    gather x1, local copies, waits for them, and re-layouts, body(): ordered = jnp.take(genotypes, assignment, axis=1)  8.06 us
    all_gather x2, blocking collectives, total_of_pieces(): pieces = lax.all_gather(array, axis)  7.53 us
    another operation x3, other arithmetic, body(): factor = jnp.linalg.cholesky(gram_sum)  6.52 us
    another operation x2, other arithmetic, body(): new_basis = jax.scipy.linalg.solve_triangular(factor, image, lower=True)  6.16 us
    split x7, local copies, waits for them, and re-layouts, body(): jnp.split(ordered, lax.axis_size('blk'), axis=1)  4.45 us
  transfers between devices with their start and end apart: 1, of which 1 were waited for; matrix products, arithmetic and copies ran while one was open for 1% of the time, Pallas kernels for 0%

profile of v1, /device:TPU:1, one launch (start us, length us, event | category | flops | bytes accessed | tf_op | source)
XLA Modules:
  0.0 193.1 jit_solution(16697413153739317817)
XLA Ops:
  0.6 0.8 compare_select_fusion
  1.5 0.7 compare_and_fusion
  2.2 8.1 %gather_fusion = bf16[128,8,1024]{2,0,1:T(8,128)(2,1)} fusion(bf16[8,128,1024]{2,1,0:T(8,128)(2,1)S(1)} %copy-done, s32[1024]{0:T(1024)S(1)} %pad_clamp_fusion), kind=kCustom, calls=%fused_computation | custom fusion | bytes 4194816 | tf_op jit(solution)/shard_map/jit(_take)/gather | solution.py:16
  10.3 1.8 select_bitcast_fusion
  12.6 0.7 fusion.48
  13.3 0.7 fusion.47
  14.0 0.7 fusion.46
  14.7 0.7 fusion.45
  15.3 0.6 fusion.44
  16.0 0.7 fusion.43
  18.5 0.6 constant_dynamic-update-slice_fusion.124
  25.1 0.6 constant_dynamic-update-slice_fusion.113
  28.2 0.6 constant_dynamic-update-slice_fusion.108
  52.5 0.6 constant_dynamic-update-slice_fusion.68
  67.0 0.6 constant_dynamic-update-slice_fusion.44
  84.0 0.6 constant_dynamic-update-slice_fusion.16
  88.3 0.6 constant_dynamic-update-slice_fusion.9
  94.3 17.0 %all-to-all-start = ((bf16[128,8,1,1024]{3,1,2,0:T(8,128)(2,1)}), bf16[128,8,1,1024]{3,1,2,0:T(8,128)(2,1)}, u32[]{:S(2)}, u32[]{:S(2)}) async-start(bf16[128,8,1,1024]{3,1,2,0:T(8,128)(2,1)} %constant_dynamic-update-slice_fusion), calls=%async_computation | async-start | bytes 4194304 | tf_op jit(solution)/shard_map/all_to_all | solution.py:18
  111.9 1.3 fusion.40
  113.2 0.7 add_compare_fusion
  113.9 46.5 %all-to-all-done = bf16[128,8,1,1024]{3,1,2,0:T(8,128)(2,1)} async-done(((bf16[128,8,1,1024]{3,1,2,0:T(8,128)(2,1)}), bf16[128,8,1,1024]{3,1,2,0:T(8,128)(2,1)}, u32[]{:S(2)}, u32[]{:S(2)}) %all-to-all-start) | async-done | bytes 2097184 | tf_op jit(solution)/shard_map/all_to_all | solution.py:18
  160.3 2.0 %convert_reduce_fusion = f32[1024]{0:T(1024)S(1)} fusion(bf16[128,8,1,1024]{3,1,2,0:T(8,128)(2,1)} %all-to-all-done), kind=kLoop, calls=%fused_computation.3 | loop fusion | flops 2096128 | bytes 2101248 | tf_op jit(solution)/shard_map/reduce_sum | solution.py:32
  162.3 2.2 %fusion.6 = f32[1024]{0:T(1024)S(1)} fusion(bf16[128,8,1,1024]{3,1,2,0:T(8,128)(2,1)} %all-to-all-done, f32[1024]{0:T(1024)S(1)} %broadcast_multiply_fusion), kind=kLoop, calls=%fused_computation.11 | loop fusion | flops 4193280 | bytes 2105344 | tf_op jit(solution)/shard_map/reduce_sum | solution.py:34
  164.5 3.6 %fusion.21 = f32[64,1024]{1,0:T(8,128)S(1)} fusion(bf16[128,8,1,1024]{3,1,2,0:T(8,128)(2,1)} %all-to-all-done, f32[1024]{0:T(1024)S(1)} %add_rsqrt_fusion, f32[1024]{0:T(1024)S(1)} %broadcast_multiply_fusion, pred[1024]{0:T(1024)(128)(4,1)S(1)} %add_compare_fusion, f32[1,64,1024]{2,1,0:T(8,128)S(1)} %copy-done.2), kind=kOutput, calls=%fused_computation.26 | convolution fusion | flops 810549248 | bytes 2630656 | tf_op jit(solution)/shard_map/nbi,bri->brn/dot_general | solution.py:39
  168.1 5.7 %all-gather = f32[128,1024]{1,0:T(8,128)S(1)} all-gather(f32[64,1024]{1,0:T(8,128)S(1)} %fusion.21), channel_id=2, replica_groups=mesh['blk'=128,'row'=2] {'row'}, dimensions={0}, use_global_device_ids=true | all-gather | bytes 786432 | tf_op jit(solution)/shard_map/all_gather | solution.py:11
  173.8 3.0 %fusion.30 = f32[1,64,1024]{2,1,0:T(8,128)S(1)} fusion(f32[64,1024]{1,0:T(8,128)S(1)} %reduce.16, bf16[128,8,1,1024]{3,1,2,0:T(8,128)(2,1)} %all-to-all-done, f32[1024]{0:T(1024)S(1)} %add_rsqrt_fusion, f32[1024]{0:T(1024)S(1)} %broadcast_multiply_fusion, pred[1024]{0:T(1024)(128)(4,1)S(1)} %add_compare_fusion, f32[1,64,1024]{2,1,0:T(8,128)S(1)} %copy-done.2), kind=kOutput, calls=%fused_computation.29 | convolution fusion | flops 810811392 | bytes 2892800 | tf_op jit(solution)/shard_map/nbi,brn->bri/dot_general | solution.py:48
  177.2 1.9 all-gather.1
  179.3 5.8 %custom-call.8 = f32[1,64,64]{2,1,0:T(8,128)S(1)} custom-call(f32[1,64,64]{2,1,0:T(8,128)S(1)} %fusion.37), custom_call_target="Cholesky" | custom-call | tf_op jit(solution)/shard_map/jit(cholesky)/cholesky | solution.py:62
  185.2 0.6 compare_reduce_fusion
  185.8 1.3 fusion.39
  187.1 4.9 %custom-call.9 = f32[1,64,64]{1,2,0:T(8,128)S(1)} custom-call(f32[1,64,64]{2,1,0:T(8,128)S(1)} %get-tuple-element.3), custom_call_target="InvertDiagBlocksLowerTriangular" | custom-call | tf_op jit(solution)/shard_map/jit(_solve_triangular)/triangular_solve | solution.py:63
  192.0 1.1 convolution_bitcast_fusion
  (143 shorter events, 75.1 us)
Async XLA Ops:
  0.6 1.6 copy-start
  94.3 17.0 %copy-start.3 = (s32[128]{0:T(128)S(1)}, s32[128]{0:T(128)}, u32[]{:S(2)}) copy-start(s32[128]{0:T(128)} %param.5) | copy-start | bytes 1540
  94.3 17.6 %copy-start.4 = (s32[128]{0:T(128)S(1)}, s32[128]{0:T(128)}, u32[]{:S(2)}) copy-start(s32[128]{0:T(128)} %param.6) | copy-start | bytes 1540
  94.3 66.0 %all-to-all-start = ((bf16[128,8,1,1024]{3,1,2,0:T(8,128)(2,1)}), bf16[128,8,1,1024]{3,1,2,0:T(8,128)(2,1)}, u32[]{:S(2)}, u32[]{:S(2)}) async-start(bf16[128,8,1,1024]{3,1,2,0:T(8,128)(2,1)} %constant_dynamic-update-slice_fusion), calls=%async_computation | async-start | bytes 4194304 | tf_op jit(solution)/shard_map/all_to_all | solution.py:18
  113.9 50.7 %copy-start.2 = (f32[1,64,1024]{2,1,0:T(8,128)S(1)}, f32[1,64,1024]{2,1,0:T(8,128)}, u32[]{:S(2)}) copy-start(f32[1,64,1024]{2,1,0:T(8,128)} %param.7) | copy-start | bytes 786436
  176.8 16.3 %copy-start.1 = (f32[1,64,1024]{2,1,0:T(8,128)}, f32[1,64,1024]{2,1,0:T(8,128)S(1)}, u32[]{:S(2)}) copy-start(f32[1,64,1024]{2,1,0:T(8,128)S(1)} %fusion.30) | copy-start | bytes 786436
